TPU v7x, 32 devices: a whole 2x2x4 slice. The times are simulated.
32 devices in a mesh: seq: 16 (over z, y, x), rep: 2 (over core).
Axes of the slice: x: 2, y: 2, z: 4, core: 2. Of those that a mesh axis runs over, the one named last changes fastest.
Arguments:
- queries: bfloat16 [4096, 4096], P(('rep', 'seq')), parts along dimension 0, may hold values from -160 to 160
- keys_values: bfloat16 [2, 4096, 1024], P(None, ('rep', 'seq')), parts along dimension 1, may hold values from -6 to 6
- segment_ids: int32 [4096], P(('rep', 'seq')), parts along dimension 0, may hold values from 0 to 31, never falling along the last dimension, each value on 1 to 1024 neighbouring positions
Outputs:
- attended: bfloat16 [4096, 4096], P(('rep', 'seq')), parts along dimension 0
There are 2 independent parts, one for each index of `rep`. A program takes and returns all parts, laid end to end along the dimension named above; each array names one. Nothing has to cross between parts.
Inputs may be any that keep to these rules, and one draw needn't show every extreme that they name: `segment_ids`: ids never fall along the tokens; every document holds 1 to 1024 consecutive tokens, one exactly 1024.
All inputs are finite; a program needn't handle non-finite values.
Results may differ from a plain program's by a relative error of at most 0.004.
Values may be sent and summed in bfloat16 or wider, within the bound.
A program may use at most 192 MiB of HBM per device.

v0:
```python
import jax
import jax.numpy as jnp
from jax import lax
from jax.sharding import PartitionSpec as P

HQ = 32
HK = 8
DH = 128
WINDOW = 2048


NEG_BIG = -1e30


def local(queries, keys_values, segment_ids):
    shard_rows = queries.shape[0]
    group_size = HQ // HK
    score_scale = DH ** (-0.5)
    offset = lax.axis_index("seq") * shard_rows
    row_index = jnp.arange(shard_rows, dtype=jnp.int32)
    query_index = offset + row_index
    id_row = segment_ids.astype(jnp.bfloat16).reshape(1, shard_rows)
    query_ids = id_row[0]
    grouped = queries.reshape(shard_rows, HK, group_size, DH)

    def attend(running, block, key_first):
        run_max, run_sum, run_acc = running
        pair, key_ids = block
        key_block = pair[0].reshape(shard_rows, HK, DH)
        value_block = pair[1].reshape(shard_rows, HK, DH)
        scores = (
            jnp.einsum("qhgd,khd->hgqk", grouped, key_block, preferred_element_type=jnp.float32)
            * score_scale
        )
        key_index = key_first + row_index
        distance = query_index[:, None] - key_index[None, :]
        keep_mask = (
            (query_ids[:, None] == key_ids[0][None, :])
            & (distance >= 0)
            & (distance < WINDOW)
            & (key_index[None, :] >= 0)
        )
        scores = jnp.where(keep_mask, scores, NEG_BIG)
        new_max = jnp.maximum(run_max, jnp.max(scores, axis=-1))
        weights = jnp.where(keep_mask, jnp.exp(scores - new_max[..., None]), 0.0)
        rescale = jnp.exp(run_max - new_max)
        new_sum = run_sum * rescale + jnp.sum(weights, axis=-1)
        new_acc = run_acc * rescale[..., None] + jnp.einsum(
            "hgqk,khd->hgqd",
            weights.astype(jnp.bfloat16),
            value_block,
            preferred_element_type=jnp.float32,
        )
        return (new_max, new_sum, new_acc)

    def visit(running, block, key_first):
        return attend(running, block, key_first)

    initial = (
        jnp.full((HK, group_size, shard_rows), NEG_BIG, jnp.float32),
        jnp.zeros((HK, group_size, shard_rows), jnp.float32),
        jnp.zeros((HK, group_size, shard_rows, DH), jnp.float32),
    )
    incoming = (
        lax.all_gather(keys_values, "seq", axis=1, tiled=True),
        lax.all_gather(id_row, "seq", axis=1, tiled=True),
    )

    def inner_step(position, state):
        start = position * shard_rows
        block = (
            lax.dynamic_slice_in_dim(incoming[0], start, shard_rows, 1),
            lax.dynamic_slice_in_dim(incoming[1], start, shard_rows, 1),
        )
        return visit(state, block, start)

    running = lax.fori_loop(0, incoming[0].shape[1] // shard_rows, inner_step, initial)
    run_max, run_sum, run_acc = running
    result = run_acc / run_sum[..., None]
    return jnp.transpose(result, (2, 0, 1, 3)).reshape(shard_rows, HQ * DH).astype(jnp.bfloat16)


def solution(mesh):
    return jax.shard_map(
        local,
        mesh=mesh,
        in_specs=(P(("rep", "seq"), None), P(None, ("rep", "seq"), None), P(("rep", "seq"))),
        out_specs=P(("rep", "seq"), None),
        check_vma=False,
    )
```

profile of v0, /device:TPU:16, one launch (start us, length us, event | category | flops | bytes accessed | tf_op | source)
XLA Modules:
  0.0 235.1 jit_solution(7376780042236925895)
XLA Ops:
  6.5 2.2 copy.16
  8.8 1.3 copy.17
  10.1 1.6 copy.18
  11.7 33.7 %all-gather.1 = bf16[16,1,128]{2,1,0:T(2,128)(2,1)S(1)} all-gather(bf16[1,1,128]{2,1,0:T(2,128)(2,1)S(1)} %get-tuple-element.256), channel_id=2, replica_groups=mesh['seq'=16,'rep'=2] {'seq'}, dimensions={0}, use_global_device_ids=true | all-gather | bytes 4352 | tf_op jit(solution)/shard_map/all_gather | solution.py:66
  45.4 106.7 %all-gather.4.cloned.1.call-done = bf16[2,2048,1024]{1,2,0:T(8,128)(2,1)} async-done(((bf16[2,128,1024]{1,2,0:T(8,128)(2,1)}), bf16[2,2048,1024]{1,2,0:T(8,128)(2,1)}) %all-gather.4.cloned.1.call-update) | async-done | bytes 8388624 | tf_op jit(solution)/shard_map/all_gather | solution.py:65
  152.1 73.0 %while.18 = (s32[]{:T(128)}, f32[8,4,128]{2,1,0:T(4,128)S(1)}, f32[8,4,128]{2,1,0:T(4,128)S(1)}, f32[8,4,128,128]{3,2,1,0:T(8,128)S(1)}, bf16[128]{0:T(256)(128)...) while((s32[]{:T(128)}, f32[8,4,128]{2,1,0:T(4,128)S(1)}, ...), condition=%wide.region_3.4_spmd.clone, body=%wide.region_0.3_spmd.clone.sunk | while | flops 276992512 | bytes 13438443 | solution.py:77
  152.3 1.1 constant_dynamic-slice_fusion.4
  154.5 2.1 fusion.45
  159.1 2.1 fusion.45
  161.4 1.1 constant_dynamic-slice_fusion.4
  163.6 2.1 fusion.45
  165.9 1.1 constant_dynamic-slice_fusion.4
  168.2 2.1 fusion.45
  172.7 2.1 fusion.45
  175.1 1.1 constant_dynamic-slice_fusion.4
  177.3 2.1 fusion.45
  179.6 1.1 constant_dynamic-slice_fusion.4
  181.9 2.1 fusion.45
  186.4 2.1 fusion.45
  191.0 2.1 fusion.45
  193.3 1.1 constant_dynamic-slice_fusion.4
  195.6 2.1 fusion.45
  200.1 2.1 fusion.45
  202.4 1.1 constant_dynamic-slice_fusion.4
  204.7 2.1 fusion.45
  207.0 1.1 constant_dynamic-slice_fusion.4
  209.2 2.1 fusion.45
  211.6 1.1 constant_dynamic-slice_fusion.4
  213.8 2.1 fusion.45
  218.4 2.1 fusion.45
  222.9 2.1 fusion.45
  226.6 1.6 convert_element_type.22
  (163 shorter events, 29.8 us)
Async XLA Ops:
  6.5 2.2 copy-start
  6.5 145.6 %all-gather.4.cloned.1.call-start = ((), (), s32[]{:S(2)}) async-start(), calls=%async_computation | async-start | bytes 8912896 | tf_op jit(solution)/shard_map/all_gather | solution.py:65
  8.8 2.9 %copy-start.1 = (s32[128]{0:T(128)S(1)}, s32[128]{0:T(128)}, u32[]{:S(2)}) copy-start(s32[128]{0:T(128)} %param.7) | copy-start | bytes 1540
Sparse Core Ops, SparseCore 0:
  10.0 142.0 all-gather.3
where the time goes:
time: 238 us; the launch traced here: 235 us
  waiting for transfers between devices  107 us (45%)
  matrix products  42.4 us (18%)
  blocking collectives  33.7 us (14%)
  local copies, waits for them, and re-layouts  25 us (11%)
  between operations  13.5 us (6%)
  other arithmetic  12.5 us (5%)
    all_gather x1, waiting for transfers between devices, local(): lax.all_gather(keys_values, 'seq', axis=1, tiled=True)  107 us
    dot_general x16, matrix products, attend(): jnp.einsum('hgqk,khd->hgqd', weights.astype(jnp.bfloat16), value_block, p...  33.7 us
    all_gather x1, blocking collectives, local(): lax.all_gather(id_row, 'seq', axis=1, tiled=True)  33.7 us
    slice x16, local copies, waits for them, and re-layouts, attend(): value_block = pair[1].reshape(shard_rows, HK, DH)  17.3 us
    reduce_sum x16, other arithmetic, attend(): new_sum = run_sum * rescale + jnp.sum(weights, axis=-1)  9.08 us
    dot_general x16, matrix products, attend(): jnp.einsum('qhgd,khd->hgqk', grouped, key_block, preferred_element_type=j...  8.7 us
    unnamed x7, local copies, waits for them, and re-layouts  5.1 us
  transfers between devices with their start and end apart: 1, of which 1 were waited for; matrix products, arithmetic and copies ran while one was open for 1% of the time, Pallas kernels for 0%

commit v1 on v0

v1 whole, which is shorter than its diff:
```python
import functools
import math

import jax
import jax.numpy as jnp
from jax import lax
from jax.experimental import pallas as pl
from jax.experimental.pallas import tpu as pltpu
from jax.sharding import PartitionSpec as P

HQ = 32
HK = 8
DH = 128
WINDOW = 2048
GROUP = HQ // HK
SPAN = 4
CHUNKS = 4
PER = HK // CHUNKS
NEG_BIG = -1e30
SCALE2 = DH ** (-0.5) * math.log2(math.e)


def kernel(n, rows, back, q_hbm, kv_hbm, ids_hbm, out_hbm, buf, ids_buf, q_buf, out_buf, bias, run_max, run_sum, run_acc,
           in_sem, out_sem, send_sem, recv_sem):
    last = back // SPAN
    planes = n // SPAN
    me = lax.axis_index("seq")
    plane = me // SPAN
    spot = me % SPAN
    low, high = spot % 2, spot // 2
    spot_x = (1 - low) + 2 * high
    spot_y = low + 2 * (1 - high)
    spot_d = (1 - low) + 2 * (1 - high)
    spots = (spot, spot_x, spot_y, spot_d)
    dev_x = plane * SPAN + spot_x
    dev_y = plane * SPAN + spot_y
    up_ok = plane < planes - 1
    down_ok = plane > 0
    dev_up = jnp.where(up_ok, me + SPAN, me - SPAN)
    dev_down = jnp.where(down_ok, me - SPAN, me + SPAN)
    ids_piece = CHUNKS

    def need(s, to, block):
        gap = SPAN * s + to - block
        return (plane >= s) & (gap >= 1) & (gap <= back)

    def via_x(s, block, c):
        mixed = (block % 2) != (block // 2)
        first = c < CHUNKS // 2 or c == ids_piece
        middle = 0 < s < last
        if first and middle:
            return block >= 0
        if first:
            return jnp.logical_not(mixed)
        if middle:
            return mixed
        return block < 0

    def ref_of(s, r, c):
        if c == ids_piece:
            return ids_buf.at[s, r]
        return buf.at[s, pl.ds(c * PER, PER), :, r]

    def copy(s, r, c, lane, to_s, to_r, device):
        return pltpu.make_async_remote_copy(
            src_ref=ref_of(s, r, c),
            dst_ref=ref_of(to_s, to_r, c),
            send_sem=send_sem.at[s, lane, c],
            recv_sem=recv_sem.at[to_s, to_r, c],
            device_id={"seq": device},
            device_id_type=pl.DeviceIdType.MESH,
        )

    def forwards(s, c):
        out = [
            (need(s, spot_x, spot), copy(s, 0, c, 0, s, 1, dev_x)),
            (need(s, spot_y, spot), copy(s, 0, c, 1, s, 2, dev_y)),
        ]
        if s < last:
            out.insert(0, (up_ok & (plane >= s), copy(s, 0, c, 2, s + 1, 0, dev_up)))
        return out

    def relay_x(s, c):
        return (need(s, spot_y, spot_x) & via_x(s, spot_x, c), copy(s, 1, c, 3, s, 3, dev_y))

    def relay_y(s, c):
        return (need(s, spot_x, spot_y) & jnp.logical_not(via_x(s, spot_y, c)), copy(s, 2, c, 4, s, 3, dev_x))

    def start(pair):
        @pl.when(pair[0])
        def _():
            pair[1].start()

    def wait_in(s, r, c):
        cond = (plane >= s) if r == 0 else need(s, spot, spots[r])

        @pl.when(cond)
        def _():
            copy(s, r, c, 0, s, r, dev_x).wait_recv()

    kv_in = [
        pltpu.make_async_copy(kv_hbm.at[:, :, pl.ds(h * DH, DH)], buf.at[0, h, :, 0], in_sem.at[h]) for h in range(HK)
    ]
    ids_in = pltpu.make_async_copy(ids_hbm, ids_buf.at[0, 0], in_sem.at[HK])
    q_in = pltpu.make_async_copy(q_hbm, q_buf, in_sem.at[HK + 1])
    ids_in.start()
    for one in kv_in:
        one.start()
    q_in.start()

    barrier = pltpu.get_barrier_semaphore()
    for cond, device in ((None, dev_x), (None, dev_y), (up_ok, dev_up), (down_ok, dev_down)):
        def greet(device=device):
            pl.semaphore_signal(barrier, inc=1, device_id={"seq": device}, device_id_type=pl.DeviceIdType.MESH)
        if cond is None:
            greet()
        else:
            pl.when(cond)(greet)
    pl.semaphore_wait(barrier, 2 + up_ok.astype(jnp.int32) + down_ok.astype(jnp.int32))

    pieces = [ids_piece] + list(range(CHUNKS))
    for c in pieces:
        if c == ids_piece:
            ids_in.wait()
        else:
            for h in range(c * PER, (c + 1) * PER):
                kv_in[h].wait()
        for pair in forwards(0, c):
            start(pair)

    for s in range(last + 1):
        for r in range(SPAN):
            if s == 0 and r == 0:
                continue
            absent = (plane < s) if r == 0 else jnp.logical_not(need(s, spot, spots[r]))

            @pl.when(absent)
            def _():
                ids_buf[s, r] = jnp.zeros((1, rows), jnp.int32)

                def clear(h, carry):
                    for k in range(2):
                        buf[s, h, k, r] = jnp.zeros((rows, DH), buf.dtype)
                    return carry

                lax.fori_loop(0, HK, clear, 0)

    q_in.wait()

    def make_bias(s):
        own = jnp.broadcast_to(ids_buf[0, 0].astype(jnp.float32), (rows, rows)).T
        row = lax.broadcasted_iota(jnp.int32, (rows, rows), 0)
        col = lax.broadcasted_iota(jnp.int32, (rows, rows), 1)
        for r in range(SPAN):
            gap = SPAN * s + spot - spots[r]
            limit = jnp.where((plane >= s) & (gap <= back), WINDOW, 0)
            distance = gap * rows + row - col
            other = jnp.broadcast_to(ids_buf[s, r].astype(jnp.float32), (rows, rows))
            allowed = (own == other) & (distance >= 0) & (distance < limit)
            bias[s, :, r * rows:(r + 1) * rows] = jnp.where(allowed, 0.0, NEG_BIG)

    def attend(s, h):
        cols = pl.ds(pl.multiple_of(h * GROUP * DH, GROUP * DH), GROUP * DH)
        wide = q_buf[:, cols]
        q = jnp.concatenate([wide[:, g * DH:(g + 1) * DH] for g in range(GROUP)], axis=0)
        k = buf[s, h, 0].reshape(SPAN * rows, DH)
        v = buf[s, h, 1].reshape(SPAN * rows, DH)
        t = lax.dot_general(q, k, (((1,), (1,)), ((), ())), preferred_element_type=jnp.float32)
        t = (t * SCALE2).reshape(GROUP, rows, SPAN * rows) + bias[s][None]
        t = t.reshape(GROUP * rows, SPAN * rows)
        top = jnp.max(t, axis=1, keepdims=True)
        if s > 0:
            old = run_max[h]
            new = jnp.maximum(old, top)
        else:
            new = jnp.broadcast_to(top, (GROUP * rows, DH))
        p = [jnp.exp2(t[:, r * rows:(r + 1) * rows] - new) for r in range(SPAN)]
        total = (p[0] + p[1]) + (p[2] + p[3])
        w = jnp.concatenate([one.astype(jnp.bfloat16) for one in p], axis=1)
        acc = jnp.dot(w, v, preferred_element_type=jnp.float32)
        if s > 0:
            fix = jnp.exp2(old - new)
            total = total + run_sum[h] * fix
            acc = acc + run_acc[h] * fix
        if s < last:
            run_max[h] = new
            run_sum[h] = total
            run_acc[h] = acc
        else:
            o = (acc / jnp.sum(total, axis=1, keepdims=True)).astype(out_buf.dtype)
            out_buf[:, cols] = jnp.concatenate([o[g * rows:(g + 1) * rows] for g in range(GROUP)], axis=1)

    def out_copy(c):
        cols = pl.ds(c * PER * GROUP * DH, PER * GROUP * DH)
        return pltpu.make_async_copy(out_buf.at[:, cols], out_hbm.at[:, cols], out_sem.at[c])

    def consume(s, c):
        wait_in(s, 3, c)
        if c == ids_piece:
            make_bias(s)
            return

        def body(h, carry):
            attend(s, h)
            return carry

        lax.fori_loop(c * PER, (c + 1) * PER, body, 0)
        if s == last:
            out_copy(c).start()

    late = None
    for s in range(last + 1):
        for c in pieces:
            if s < last:
                wait_in(s + 1, 0, c)
                for pair in forwards(s + 1, c):
                    start(pair)
            wait_in(s, 1, c)
            start(relay_x(s, c))
            wait_in(s, 2, c)
            start(relay_y(s, c))
            if late is not None:
                consume(*late)
            late = (s, c)
    consume(*late)

    for s in range(last + 1):
        for c in pieces:
            for cond, one in forwards(s, c) + [relay_x(s, c), relay_y(s, c)]:
                @pl.when(cond)
                def _():
                    one.wait_send()
    for c in range(CHUNKS):
        out_copy(c).wait()


def solution(mesh):
    n = mesh.shape["seq"]

    def local(queries, keys_values, segment_ids):
        rows = queries.shape[0]
        reach = min(WINDOW, n * rows // 2)
        back = -(-(reach - 1) // rows)
        assert n % SPAN == 0 and back % SPAN == 0
        sets = back // SPAN + 1
        group_rows = GROUP * rows
        return pl.pallas_call(
            functools.partial(kernel, n, rows, back),
            out_shape=jax.ShapeDtypeStruct(queries.shape, queries.dtype),
            in_specs=[pl.BlockSpec(memory_space=pl.ANY)] * 3,
            out_specs=pl.BlockSpec(memory_space=pl.ANY),
            scratch_shapes=[
                pltpu.VMEM((sets, HK, 2, SPAN, rows, DH), jnp.bfloat16),
                pltpu.VMEM((sets, SPAN, 1, rows), jnp.int32),
                pltpu.VMEM((rows, HQ * DH), jnp.bfloat16),
                pltpu.VMEM((rows, HQ * DH), jnp.bfloat16),
                pltpu.VMEM((sets, rows, SPAN * rows), jnp.float32),
                pltpu.VMEM((HK, group_rows, DH), jnp.float32),
                pltpu.VMEM((HK, group_rows, DH), jnp.float32),
                pltpu.VMEM((HK, group_rows, DH), jnp.float32),
                pltpu.SemaphoreType.DMA((HK + 2,)),
                pltpu.SemaphoreType.DMA((CHUNKS,)),
                pltpu.SemaphoreType.DMA((sets, 5, CHUNKS + 1)),
                pltpu.SemaphoreType.DMA((sets, SPAN, CHUNKS + 1)),
            ],
            compiler_params=pltpu.CompilerParams(
                collective_id=0, has_side_effects=True, vmem_limit_bytes=60 * 1024 * 1024
            ),
        )(queries, keys_values, segment_ids.reshape(1, rows))

    return jax.shard_map(
        local,
        mesh=mesh,
        in_specs=(P(("rep", "seq"), None), P(None, ("rep", "seq"), None), P(("rep", "seq"))),
        out_specs=P(("rep", "seq"), None),
        check_vma=False,
    )
```

time: 238 us -> 75.1 us (0.32); the launches traced: 235 us -> 75 us
  waiting for transfers between devices: 107 us -> 0 us
  Pallas kernels: 0 us -> 72.7 us
  matrix products: 42.4 us -> 0 us
  blocking collectives: 33.7 us -> 0 us
  local copies, waits for them, and re-layouts: 25 us -> 2.29 us
  between operations: 13.5 us -> 0.01 us
  other arithmetic: 12.5 us -> 0 us
    all_gather x1 -> x0, waiting for transfers between devices: 107 us -> none  [local(): lax.all_gather(keys_values, 'seq', axis=1, tiled=True)]
    pallas_call x0 -> x1, Pallas kernels: none -> 72.7 us  [local(): pl.pallas_call(functools.partial(kernel, n, rows, back), out_shape=jax.Sh...]
    dot_general x32 -> x0, matrix products: 42.4 us -> none  [the longest x16 33.7 us: attend(): jnp.einsum('hgqk,khd->hgqd', weights.astype(jnp.bfloat16), value_block, p...]
    all_gather x1 -> x0, blocking collectives: 33.7 us -> none  [local(): lax.all_gather(id_row, 'seq', axis=1, tiled=True)]
    slice x16 -> x0, local copies, waits for them, and re-layouts: 17.3 us -> none  [attend(): value_block = pair[1].reshape(shard_rows, HK, DH)]
    reduce_sum x16 -> x0, other arithmetic: 9.08 us -> none  [attend(): new_sum = run_sum * rescale + jnp.sum(weights, axis=-1)]
    unnamed x7 -> x1, local copies, waits for them, and re-layouts: 5.1 us -> 2.29 us
    convert_element_type x2 -> x0, local copies, waits for them, and re-layouts: 2.42 us -> none  [local(): jnp.transpose(result, (2, 0, 1, 3)).reshape(shard_rows, HQ * DH)]
  transfers between devices with their start and end apart: 1 -> 0, of which waited for: 1 -> 0; matrix products, arithmetic and copies ran while one was open for 1% -> 0% of each run, Pallas kernels for 0% -> 0%
where the time goes in v1:
time: 75.1 us; the launch traced here: 75 us
  Pallas kernels  72.7 us (97%)
  local copies, waits for them, and re-layouts  2.29 us (3%)
    pallas_call x1, Pallas kernels, local(): pl.pallas_call(functools.partial(kernel, n, rows, back), out_shape=jax.Sh...  72.7 us
    unnamed x1, local copies, waits for them, and re-layouts  2.29 us

profile of v1, /device:TPU:16, one launch (start us, length us, event | category | flops | bytes accessed | tf_op | source)
XLA Modules:
  0.0 75.0 jit_solution(580883770006337766)
XLA Ops:
  0.0 72.7 %shard_map.37 = bf16[128,4096]{1,0:T(8,128)(2,1)} custom-call(bf16[128,4096]{1,0:T(8,128)(2,1)} %q_hbm.1, bf16[2,128,1024]{2,1,0:T(8,128)(2,1)} %kv_hbm.1, s32[1,128]{1,0:T(1,128)} %bitcast.1), custom_call_target="tpu_custom_call" | custom-call | tf_op jit(solution)/shard_map/pallas_call | solution.py:247
  72.7 2.3 %copy.5 = bf16[128,4096]{1,0:T(8,128)(2,1)} copy(bf16[128,4096]{1,0:T(8,128)(2,1)} %shard_map.37) | data formatting | bytes 2097152

commit v2 on v1

--- a/solution.py
+++ b/solution.py
@@ -14,7 +14,8 @@
 WINDOW = 2048
 GROUP = HQ // HK
 SPAN = 4
-CHUNKS = 4
+CHUNKS = 8
+RELAY_LAG, USE_LAG, LAST_LAG, TAIL_LAG = 4, 13, 6, 11
 PER = HK // CHUNKS
 NEG_BIG = -1e30
 SCALE2 = DH ** (-0.5) * math.log2(math.e)
@@ -147,11 +148,11 @@
 
     q_in.wait()
 
-    def make_bias(s):
+    def make_bias(s, begin, end):
         own = jnp.broadcast_to(ids_buf[0, 0].astype(jnp.float32), (rows, rows)).T
         row = lax.broadcasted_iota(jnp.int32, (rows, rows), 0)
         col = lax.broadcasted_iota(jnp.int32, (rows, rows), 1)
-        for r in range(SPAN):
+        for r in range(begin, end):
             gap = SPAN * s + spot - spots[r]
             limit = jnp.where((plane >= s) & (gap <= back), WINDOW, 0)
             distance = gap * rows + row - col
@@ -159,70 +160,83 @@
             allowed = (own == other) & (distance >= 0) & (distance < limit)
             bias[s, :, r * rows:(r + 1) * rows] = jnp.where(allowed, 0.0, NEG_BIG)
 
-    def attend(s, h):
+    def attend(s, h, begin, end):
+        first, final = s == 0, s == last and end == SPAN
+        span = (end - begin) * rows
         cols = pl.ds(pl.multiple_of(h * GROUP * DH, GROUP * DH), GROUP * DH)
         wide = q_buf[:, cols]
         q = jnp.concatenate([wide[:, g * DH:(g + 1) * DH] for g in range(GROUP)], axis=0)
-        k = buf[s, h, 0].reshape(SPAN * rows, DH)
-        v = buf[s, h, 1].reshape(SPAN * rows, DH)
+        k = buf[s, h, 0, begin:end].reshape(span, DH)
+        v = buf[s, h, 1, begin:end].reshape(span, DH)
         t = lax.dot_general(q, k, (((1,), (1,)), ((), ())), preferred_element_type=jnp.float32)
-        t = (t * SCALE2).reshape(GROUP, rows, SPAN * rows) + bias[s][None]
-        t = t.reshape(GROUP * rows, SPAN * rows)
+        t = (t * SCALE2).reshape(GROUP, rows, span) + bias[s, :, begin * rows:end * rows][None]
+        t = t.reshape(GROUP * rows, span)
         top = jnp.max(t, axis=1, keepdims=True)
-        if s > 0:
+        if first:
+            new = jnp.broadcast_to(top, (GROUP * rows, DH))
+        else:
             old = run_max[h]
             new = jnp.maximum(old, top)
-        else:
-            new = jnp.broadcast_to(top, (GROUP * rows, DH))
-        p = [jnp.exp2(t[:, r * rows:(r + 1) * rows] - new) for r in range(SPAN)]
-        total = (p[0] + p[1]) + (p[2] + p[3])
+        p = [jnp.exp2(t[:, r * rows:(r + 1) * rows] - new) for r in range(end - begin)]
+        total = functools.reduce(lambda x, y: x + y, p)
         w = jnp.concatenate([one.astype(jnp.bfloat16) for one in p], axis=1)
         acc = jnp.dot(w, v, preferred_element_type=jnp.float32)
-        if s > 0:
+        if not first:
             fix = jnp.exp2(old - new)
             total = total + run_sum[h] * fix
             acc = acc + run_acc[h] * fix
-        if s < last:
+        if final:
+            o = (acc / jnp.sum(total, axis=1, keepdims=True)).astype(out_buf.dtype)
+            out_buf[:, cols] = jnp.concatenate([o[g * rows:(g + 1) * rows] for g in range(GROUP)], axis=1)
+        else:
             run_max[h] = new
             run_sum[h] = total
             run_acc[h] = acc
-        else:
-            o = (acc / jnp.sum(total, axis=1, keepdims=True)).astype(out_buf.dtype)
-            out_buf[:, cols] = jnp.concatenate([o[g * rows:(g + 1) * rows] for g in range(GROUP)], axis=1)
 
     def out_copy(c):
         cols = pl.ds(c * PER * GROUP * DH, PER * GROUP * DH)
         return pltpu.make_async_copy(out_buf.at[:, cols], out_hbm.at[:, cols], out_sem.at[c])
 
-    def consume(s, c):
-        wait_in(s, 3, c)
+    def consume(s, c, begin, end):
+        if end == SPAN:
+            wait_in(s, SPAN - 1, c)
         if c == ids_piece:
-            make_bias(s)
+            make_bias(s, begin, end)
             return
 
         def body(h, carry):
-            attend(s, h)
+            attend(s, h, begin, end)
             return carry
 
         lax.fori_loop(c * PER, (c + 1) * PER, body, 0)
-        if s == last:
+        if s == last and end == SPAN:
             out_copy(c).start()
 
-    late = None
+    def pass_on(s, c):
+        wait_in(s, 0, c)
+        for pair in forwards(s, c):
+            start(pair)
+
+    def relay(s, c):
+        wait_in(s, 1, c)
+        start(relay_x(s, c))
+        wait_in(s, 2, c)
+        start(relay_y(s, c))
+
+    steps = []
     for s in range(last + 1):
-        for c in pieces:
+        for place, c in enumerate(pieces):
+            now = s * len(pieces) + place
+            if s > 0:
+                steps.append((now - len(pieces), 0, functools.partial(pass_on, s, c)))
+            steps.append((now + (RELAY_LAG if 0 < s < last else 0), 1, functools.partial(relay, s, c)))
             if s < last:
-                wait_in(s + 1, 0, c)
-                for pair in forwards(s + 1, c):
-                    start(pair)
-            wait_in(s, 1, c)
-            start(relay_x(s, c))
-            wait_in(s, 2, c)
-            start(relay_y(s, c))
-            if late is not None:
-                consume(*late)
-            late = (s, c)
-    consume(*late)
+                steps.append((now + USE_LAG, 2, functools.partial(consume, s, c, 0, SPAN)))
+            else:
+                steps.append((now + LAST_LAG, 3, functools.partial(consume, s, c, 0, SPAN - 1)))
+                steps.append((now + TAIL_LAG, 4, functools.partial(consume, s, c, SPAN - 1, SPAN)))
+    for _, _, step in sorted(steps, key=lambda one: one[:2]):
+        step()
 
     for s in range(last + 1):
         for c in pieces:

time: 75.1 us -> 53.9 us (0.72)
  the two profiles are of different devices: /device:TPU:16 before, /device:TPU:28 now
where the time goes in v2:
time: 53.9 us; the launch traced here: 53.8 us
  Pallas kernels  51.5 us (96%)
  local copies, waits for them, and re-layouts  2.29 us (4%)
    pallas_call x1, Pallas kernels, local(): pl.pallas_call(functools.partial(kernel, n, rows, back), out_shape=jax.Sh...  51.5 us
    unnamed x1, local copies, waits for them, and re-layouts  2.29 us

profile of v2, /device:TPU:28, one launch (start us, length us, event | category | flops | bytes accessed | tf_op | source)
XLA Modules:
  0.0 53.8 jit_solution(529380570625093189)
XLA Ops:
  0.0 51.5 %shard_map.37 = bf16[128,4096]{1,0:T(8,128)(2,1)} custom-call(bf16[128,4096]{1,0:T(8,128)(2,1)} %q_hbm.1, bf16[2,128,1024]{2,1,0:T(8,128)(2,1)} %kv_hbm.1, s32[1,128]{1,0:T(1,128)} %bitcast.1), custom_call_target="tpu_custom_call" | custom-call | tf_op jit(solution)/shard_map/pallas_call | solution.py:261
  51.5 2.3 %copy.5 = bf16[128,4096]{1,0:T(8,128)(2,1)} copy(bf16[128,4096]{1,0:T(8,128)(2,1)} %shard_map.37) | data formatting | bytes 2097152
